TPU v7x, 32 devices: a whole 2x2x4 slice. The times are simulated.
32 devices in a mesh: wide: 8 (over z, core), narrow: 4 (over y, x).
Axes of the slice: x: 2, y: 2, z: 4, core: 2. Of those that a mesh axis runs over, the one named last changes fastest.
Arguments:
- points: float32 [8192, 128], P(('wide', 'narrow')), may hold values from -6 to 6
- targets: float32 [16, 8192], P(None, ('wide', 'narrow')), may hold values from -6 to 6
- start: float32 [16, 8192], P(None, ('wide', 'narrow')), may hold values from -6 to 6
- interp: float32 [8192, 128], P(('wide', 'narrow')), may hold values from -0.375 to 0.375
- skel_points: float32 [1024, 128], P('wide'), may hold values from -6 to 6
- near_leaves: int32 [64, 8], P(('wide', 'narrow')), may hold values from 0 to 7, as said below
- near_count: int32 [64], P(('wide', 'narrow')), may hold values from 1 to 8
Outputs:
- weights: float32 [16, 8192], P(None, ('wide', 'narrow'))
- residual: float32 [16, 8192], P(None, ('wide', 'narrow'))
Inputs may be any that keep to these rules, and one draw needn't show every extreme that they name: `near_leaves`: each row names 8 different leaves of the row's own subtree.
All inputs are finite; a program needn't handle non-finite values.
Results may differ from a plain program's by a relative error of at most 0.0003.
Values sent between devices are 32-bit elements; how exact they have to be, the bound alone decides.
No kernel may reach another device: no remote copies, remote signals or barrier semaphores. Data moves between devices by JAX's collectives and lax.ppermute only.
A program may use at most 64 MiB of HBM per device.

v0:
```python
import math
import jax
import jax.numpy as jnp
from jax import lax
from jax.sharding import PartitionSpec as P

ITERS = 2
ridge_shift = 1.0
step_size = 0.05
kernel_rate = 2.0
highest = lax.Precision.HIGHEST


def kernel(left_points, right_points, features):
    cross_prod = jnp.dot(
        left_points, right_points.T, precision=highest, preferred_element_type=jnp.float32
    )
    left_sq = jnp.sum(left_points * left_points, axis=1)
    right_sq = jnp.sum(right_points * right_points, axis=1)
    return jnp.exp(
        -(kernel_rate / features) * (left_sq[:, None] + right_sq[None, :] - 2.0 * cross_prod)
    )


def far_block(row_blocks, skeleton, columns, features):

    def row_group(block_points):
        kernel_vals = kernel(block_points, skeleton, features)
        return jnp.einsum("rs,ps->rp", columns, kernel_vals, precision=highest)

    pieces_out = lax.map(row_group, row_blocks)
    return jnp.transpose(pieces_out, (1, 0, 2)).reshape(columns.shape[0], -1)


def on_device(points, targets, start, interp, skel_points, near_leaves, near_count):
    leaf_dev, near_slots = near_leaves.shape
    row_total, features = points.shape
    leaf_size = row_total // leaf_dev
    rhs_count = targets.shape[0]
    skel_rank = interp.shape[1]
    block_rows = math.gcd(row_total, 512)
    row_blocks = points.reshape(row_total // block_rows, block_rows, features)
    own_blocks = points.reshape(leaf_dev, leaf_size, features)
    subtree = lax.all_gather(points, "narrow", axis=0, tiled=True).reshape(-1, leaf_size, features)
    neighbours = subtree[near_leaves]
    cross_prod = jnp.einsum("ipd,ikqd->ikpq", own_blocks, neighbours, precision=highest)
    own_sq = jnp.sum(own_blocks * own_blocks, axis=-1)
    near_sq = jnp.sum(neighbours * neighbours, axis=-1)
    live_mask = (jnp.arange(near_slots, dtype=jnp.int32)[None, :] < near_count[:, None]).astype(
        jnp.float32
    )
    distance = own_sq[:, None, :, None] + near_sq[:, :, None, :] - 2.0 * cross_prod
    near_kern = jnp.exp(-(kernel_rate / features) * distance) * live_mask[:, :, None, None]
    group_index = lax.axis_index("wide")
    weights = start
    residual = targets
    for iteration in range(ITERS):
        gathered = lax.all_gather(weights, "narrow", axis=1, tiled=True).reshape(
            rhs_count, -1, leaf_size
        )
        picked = gathered[:, near_leaves]
        near_term = jnp.einsum("ikpq,rikq->rip", near_kern, picked, precision=highest).reshape(
            rhs_count, row_total
        )
        node_local = jnp.dot(weights, interp, precision=highest, preferred_element_type=jnp.float32)
        summed = lax.psum(node_local, "narrow")
        skel_table = lax.all_gather(summed, "wide", axis=1, tiled=True)
        owner_node = jnp.arange(skel_table.shape[1], dtype=jnp.int32) // skel_rank
        skel_table = jnp.where((owner_node == group_index)[None, :], jnp.float32(0.0), skel_table)
        far_term = far_block(
            row_blocks,
            lax.all_gather(skel_points, "wide", axis=0, tiled=True),
            skel_table,
            features,
        )
        residual = targets - (ridge_shift * weights + (near_term + far_term))
        weights = weights + step_size * residual
    return (weights, residual)


def solution(mesh):
    in_specs = (
        P(("wide", "narrow"), None),
        P(None, ("wide", "narrow")),
        P(None, ("wide", "narrow")),
        P(("wide", "narrow"), None),
        P("wide", None),
        P(("wide", "narrow"), None),
        P(("wide", "narrow")),
    )
    out_specs = (P(None, ("wide", "narrow")), P(None, ("wide", "narrow")))
    return jax.shard_map(
        on_device, mesh=mesh, in_specs=in_specs, out_specs=out_specs, check_vma=False
    )
```

profile of v0, /device:TPU:0, one launch (start us, length us, event | category | flops | bytes accessed | tf_op | source)
XLA Modules:
  0.0 100.6 jit_solution(13071996611529464808)
XLA Ops:
  0.6 0.7 compare_select_fusion
  1.5 11.9 %all_gather.20 = f32[1024,128]{1,0:T(8,128)S(1)} all-gather(f32[256,128]{1,0:T(8,128)} %param.7), channel_id=1, replica_groups=mesh['wide'=8,'narrow'=4] {'narrow'}, dimensions={0}, use_global_device_ids=true | all-gather | bytes 655360 | tf_op jit(solution)/shard_map/all_gather | solution.py:44
  13.3 0.6 gather_fusion.1
  14.0 0.3 multiply_reduce_fusion
  14.3 0.5 copy-done.1
  15.0 0.6 copy-done.5
  15.7 1.2 %fusion.7 = f32[2,8,128,128]{2,3,1,0:T(8,128)S(1)} fusion(f32[2,8,128,128]{3,2,1,0:T(8,128)S(1)} %bitcast.65, f32[2,128,128,1]{2,1,3,0:T(8,128)S(1)} %bitcast.67, f32[2,8]{1,0:T(2,128)S(1)} %compare_convert_fusion, f32[2,8,128]{2,1,0:T(8,128)S(1)} %multiply_reduce_fusion, f32[2,128]{1,0:T(2,128)S(1)} %bitcast.70), kind=kOutput, calls=%fused_computation.12 | convolution fusion | flops 403963904 | bytes 2237504 | tf_op jit(solution)/shard_map/ipd,ikqd->ikpq/dot_general | solution.py:46
  16.9 7.9 %all_gather.19 = f32[16,1024]{1,0:T(8,128)S(1)} all-gather(f32[16,256]{1,0:T(8,128)S(1)} %copy-done.2), channel_id=1, replica_groups=mesh['wide'=8,'narrow'=4] {'narrow'}, dimensions={1}, use_global_device_ids=true | all-gather | bytes 81920 | tf_op jit(solution)/shard_map/all_gather | solution.py:58
  24.8 0.6 gather_fusion
  25.4 0.6 convolution_bitcast_fusion.1
  26.0 0.2 copy-done.4
  26.2 15.2 %all_gather.22 = f32[1024,128]{1,0:T(8,128)S(1)} all-gather(f32[128,128]{1,0:T(8,128)S(1)} %copy-done.4), channel_id=1, replica_groups=mesh['wide'=8,'narrow'=4] {'wide'}, dimensions={0}, use_global_device_ids=true | all-gather | bytes 589824 | tf_op jit(solution)/shard_map/all_gather | solution.py:72
  41.4 0.2 multiply_reduce_fusion.1
  41.6 1.2 %fusion.2 = f32[256,1024]{1,0:T(8,128)S(1)} fusion(f32[256,128]{1,0:T(8,128)S(1)} %copy-done.1, f32[1024,128]{1,0:T(8,128)S(1)} %all_gather.22, f32[1024]{0:T(1024)S(1)} %multiply_reduce_fusion.1, f32[256]{0:T(256)S(1)} %multiply_reduce_fusion.2), kind=kOutput, calls=%fused_computation.6 | convolution fusion | flops 403701760 | bytes 1709056 | tf_op jit(solution)/shard_map/while/body/eval_jaxpr/dot_general | solution.py:15
  43.0 9.1 %psum.14 = f32[16,128]{1,0:T(8,128)S(1)} all-reduce(f32[16,128]{1,0:T(8,128)S(1)} %fusion.26), channel_id=1, replica_groups=mesh['wide'=8,'narrow'=4] {'narrow'}, use_global_device_ids=true, to_apply=%region_2.0 | all-reduce | flops 2048 | bytes 16384 | tf_op jit(solution)/shard_map/psum | solution.py:66
  52.1 14.0 %all_gather.21 = f32[16,1024]{1,0:T(8,128)S(1)} all-gather(f32[16,128]{1,0:T(8,128)S(1)} %psum.14), channel_id=1, replica_groups=mesh['wide'=8,'narrow'=4] {'wide'}, dimensions={1}, use_global_device_ids=true | all-gather | bytes 73728 | tf_op jit(solution)/shard_map/all_gather | solution.py:67
  66.1 0.9 fusion.13
  67.0 7.6 %all_gather.23 = f32[16,1024]{1,0:T(8,128)S(1)} all-gather(f32[16,256]{1,0:T(8,128)S(1)} %fusion.13), channel_id=1, replica_groups=mesh['wide'=8,'narrow'=4] {'narrow'}, dimensions={1}, use_global_device_ids=true | all-gather | bytes 81920 | tf_op jit(solution)/shard_map/all_gather | solution.py:58
  74.6 0.6 gather_fusion.2
  75.2 0.6 convolution_bitcast_fusion
  75.8 0.2 fusion.27
  76.0 9.1 %psum.15 = f32[16,128]{1,0:T(8,128)S(1)} all-reduce(f32[16,128]{1,0:T(8,128)S(1)} %fusion.27), channel_id=1, replica_groups=mesh['wide'=8,'narrow'=4] {'narrow'}, use_global_device_ids=true, to_apply=%region_4.5 | all-reduce | flops 2048 | bytes 16384 | tf_op jit(solution)/shard_map/psum | solution.py:66
  85.1 14.0 %all_gather.24 = f32[16,1024]{1,0:T(8,128)S(1)} all-gather(f32[16,128]{1,0:T(8,128)S(1)} %psum.15), channel_id=1, replica_groups=mesh['wide'=8,'narrow'=4] {'wide'}, dimensions={1}, use_global_device_ids=true | all-gather | bytes 73728 | tf_op jit(solution)/shard_map/all_gather | solution.py:67
  99.0 1.5 %multiply_add_fusion = (f32[16,256]{1,0:T(8,128)}, f32[16,256]{1,0:T(8,128)}) fusion(f32[16,256]{1,0:T(8,128)S(1)} %fusion.13, f32[16,256]{1,0:T(8,128)S(1)} %copy-done.3, f32[256,1024]{1,0:T(8,128)S(1)} %fusion.2, f32[16,1024]{1,0:T(8,128)S(1)} %all_gather.24, pred[1024]{0:T(1024)(128)(4,1)S(1)} %fusion.20, f32[2,2,8,128]{3,2,1,0:T(8,128)S(1)} %convolution_bitcast_fusion), kind=kOutput, calls=%fused_computation.34 | convolution fusion | flops 50368512 | bytes 1197056 | tf_op jit(solution)/shard_map/while/body/eval_jaxpr/rs,ps->rp/dot_general | solution.py:29
  (17 shorter events, 0.5 us)
Async XLA Ops:
  0.6 42.2 %copy-start = (f32[256,128]{1,0:T(8,128)S(1)}, f32[256,128]{1,0:T(8,128)}, u32[]{:S(2)}) copy-start(f32[256,128]{1,0:T(8,128)} %param.10) | copy-start | bytes 393220
  13.9 0.9 copy-start.1
  15.0 0.7 copy-start.5
  15.7 1.2 %copy-start.2 = (f32[16,256]{1,0:T(8,128)S(1)}, f32[16,256]{1,0:T(8,128)}, u32[]{:S(2)}) copy-start(f32[16,256]{1,0:T(8,128)} %param.9) | copy-start | bytes 49156
  25.4 0.8 copy-start.4
  52.1 14.0 %copy-start.3 = (f32[16,256]{1,0:T(8,128)S(1)}, f32[16,256]{1,0:T(8,128)}, u32[]{:S(2)}) copy-start(f32[16,256]{1,0:T(8,128)} %param.8) | copy-start | bytes 49156
where the time goes:
time: 101 us
  blocking collectives  88.6 us (88%)
  matrix products  6.43 us (6%)
  local copies, waits for them, and re-layouts  3.27 us (3%)
  other arithmetic  1.46 us (1%)
    all_gather x2, blocking collectives, on_device(): skel_table = lax.all_gather(summed, 'wide', axis=1, tiled=True)  27.9 us
    psum x2, blocking collectives, on_device(): summed = lax.psum(node_local, 'narrow')  18.2 us
    all_gather x2, blocking collectives, on_device(): lax.all_gather(weights, 'narrow', axis=1, tiled=True)  15.5 us
    all_gather x1, blocking collectives, on_device(): lax.all_gather(skel_points, 'wide', axis=0, tiled=True)  15.2 us
    all_gather x1, blocking collectives, on_device(): lax.all_gather(points, 'narrow', axis=0, tiled=True)  11.9 us
    dot_general x2, matrix products, row_group(): return jnp.einsum('rs,ps->rp', columns, kernel_vals, precision=highest)  2.48 us

commit v1 on v0

--- a/solution.py
+++ b/solution.py
@@ -63,7 +63,9 @@
             rhs_count, row_total
         )
         node_local = jnp.dot(weights, interp, precision=highest, preferred_element_type=jnp.float32)
-        summed = lax.psum(node_local, "narrow")
+        summed = node_local
+        for hop in (1, 2):
+            summed = summed + lax.ppermute(summed, "narrow", [(dev, dev ^ hop) for dev in range(4)])
         skel_table = lax.all_gather(summed, "wide", axis=1, tiled=True)
         owner_node = jnp.arange(skel_table.shape[1], dtype=jnp.int32) // skel_rank
         skel_table = jnp.where((owner_node == group_index)[None, :], jnp.float32(0.0), skel_table)

time: 101 us -> 97.8 us (0.968)
  blocking collectives: 88.6 us -> 69.1 us
  waiting for transfers between devices: 0 us -> 7.27 us
  starting transfers between devices: 0 us -> 5.35 us
  matrix products: 6.43 us -> 7.75 us
  other arithmetic: 1.46 us -> 2.62 us
  local copies, waits for them, and re-layouts: 3.27 us -> 4.38 us
    psum x2 -> x0, blocking collectives: 18.2 us -> none  [on_device(): summed = lax.psum(node_local, 'narrow')]
    ppermute x0 -> x4, waiting for transfers between devices: none -> 7.27 us  [on_device(): lax.ppermute(summed, 'narrow', [(dev, dev ^ hop) for dev in range(4)])]
    ppermute x0 -> x4, starting transfers between devices: none -> 5.35 us  [on_device(): lax.ppermute(summed, 'narrow', [(dev, dev ^ hop) for dev in range(4)])]
    all_gather x1, blocking collectives: 11.9 us -> 10.2 us  [on_device(): lax.all_gather(points, 'narrow', axis=0, tiled=True)]
    dot_general x2, matrix products: 0.35 us -> 1.67 us  [on_device(): jnp.dot(weights, interp, precision=highest, preferred_element_type=jnp.fl...]
    unnamed x12 -> x24, local copies, waits for them, and re-layouts: 1.43 us -> 2.42 us
  transfers between devices with their start and end apart: 0 -> 4, of which waited for: 0 -> 3; matrix products, arithmetic and copies ran while one was open for 0% -> 8% of each run, Pallas kernels for 0% -> 0%
where the time goes in v1:
time: 97.8 us; the launch traced here: 97.3 us
  blocking collectives  69.1 us (71%)
  matrix products  7.75 us (8%)
  waiting for transfers between devices  7.27 us (7%)
  starting transfers between devices  5.35 us (5%)
  local copies, waits for them, and re-layouts  4.38 us (4%)
  other arithmetic  2.62 us (3%)
    all_gather x2, blocking collectives, on_device(): skel_table = lax.all_gather(summed, 'wide', axis=1, tiled=True)  28 us
    all_gather x2, blocking collectives, on_device(): lax.all_gather(weights, 'narrow', axis=1, tiled=True)  15.6 us
    all_gather x1, blocking collectives, on_device(): lax.all_gather(skel_points, 'wide', axis=0, tiled=True)  15.2 us
    all_gather x1, blocking collectives, on_device(): lax.all_gather(points, 'narrow', axis=0, tiled=True)  10.2 us
    ppermute x4, waiting for transfers between devices, on_device(): lax.ppermute(summed, 'narrow', [(dev, dev ^ hop) for dev in range(4)])  7.27 us
    ppermute x4, starting transfers between devices, on_device(): lax.ppermute(summed, 'narrow', [(dev, dev ^ hop) for dev in range(4)])  5.35 us
    dot_general x2, matrix products, row_group(): return jnp.einsum('rs,ps->rp', columns, kernel_vals, precision=highest)  2.48 us
    unnamed x24, local copies, waits for them, and re-layouts  2.42 us
  transfers between devices with their start and end apart: 4, of which 3 were waited for; matrix products, arithmetic and copies ran while one was open for 8% of the time, Pallas kernels for 0%

profile of v1, /device:TPU:0, one launch (start us, length us, event | category | flops | bytes accessed | tf_op | source)
XLA Modules:
  0.0 97.3 jit_solution(1232495998820689823)
XLA Ops:
  0.7 0.9 copy-done
  1.5 1.5 %fusion.26 = f32[16,128]{1,0:T(8,128)} fusion(f32[16,256]{1,0:T(8,128)} %param.9, f32[256,128]{1,0:T(8,128)S(1)} %copy-done), kind=kOutput, calls=%fused_computation.48 | convolution fusion | flops 6291456 | bytes 155648 | tf_op jit(solution)/shard_map/dot_general | solution.py:65
  3.0 3.0 %collective-permute-start = (f32[16,128]{1,0:T(8,128)}, f32[16,128]{1,0:T(8,128)}, u32[]{:S(2)}, u32[]{:S(2)}) collective-permute-start(f32[16,128]{1,0:T(8,128)} %fusion.26), channel_id=1, source_target_pairs={{0,1},{1,0},{2,3},{3,2},{4,5},{5,4},{6,7},{7,6},{8,9},{9,8},{10,11... | collective-permute-start | bytes 24584 | tf_op jit(solution)/shard_map/ppermute | solution.py:68
  6.0 10.2 %all_gather.20 = f32[1024,128]{1,0:T(8,128)S(1)} all-gather(f32[256,128]{1,0:T(8,128)S(1)} %copy-done.1), channel_id=1, replica_groups=mesh['wide'=8,'narrow'=4] {'narrow'}, dimensions={0}, use_global_device_ids=true | all-gather | bytes 655360 | tf_op jit(solution)/shard_map/all_gather | solution.py:44
  17.0 7.2 %all_gather.19 = f32[16,1024]{1,0:T(8,128)S(1)} all-gather(f32[16,256]{1,0:T(8,128)S(1)} %copy-done.2), channel_id=1, replica_groups=mesh['wide'=8,'narrow'=4] {'narrow'}, dimensions={1}, use_global_device_ids=true | all-gather | bytes 81920 | tf_op jit(solution)/shard_map/all_gather | solution.py:58
  24.3 0.6 gather_fusion.1
  24.9 0.9 multiply_reduce_fusion
  27.3 15.2 %all_gather.22 = f32[1024,128]{1,0:T(8,128)S(1)} all-gather(f32[128,128]{1,0:T(8,128)S(1)} %copy-done.4), channel_id=1, replica_groups=mesh['wide'=8,'narrow'=4] {'wide'}, dimensions={0}, use_global_device_ids=true | all-gather | bytes 589824 | tf_op jit(solution)/shard_map/all_gather | solution.py:74
  42.7 1.1 %fusion.2 = f32[256,1024]{1,0:T(8,128)S(1)} fusion(f32[256,128]{1,0:T(8,128)S(1)} %copy-done.1, f32[1024,128]{1,0:T(8,128)S(1)} %all_gather.22, f32[1024]{0:T(1024)S(1)} %multiply_reduce_fusion.1, f32[256]{0:T(256)S(1)} %multiply_reduce_fusion.2), kind=kOutput, calls=%fused_computation.6 | convolution fusion | flops 403701760 | bytes 1709056 | tf_op jit(solution)/shard_map/while/body/eval_jaxpr/dot_general | solution.py:15
  43.9 0.6 copy-done.8
  44.5 1.2 %fusion.7 = f32[2,8,128,128]{2,3,1,0:T(8,128)S(1)} fusion(f32[2,8,128,128]{3,2,1,0:T(8,128)S(1)} %bitcast.65, f32[2,128,128,1]{2,1,3,0:T(8,128)S(1)} %bitcast.67, f32[2,8]{1,0:T(2,128)S(1)} %copy-done.9, f32[2,8,128]{2,1,0:T(8,128)S(1)} %copy-done.5, f32[2,128]{1,0:T(2,128)S(1)} %bitcast.70), kind=kOutput, calls=%fused_computation.12 | convolution fusion | flops 403963904 | bytes 2237504 | tf_op jit(solution)/shard_map/ipd,ikqd->ikpq/dot_general | solution.py:46
  45.8 0.6 convolution_bitcast_fusion.1
  46.4 0.7 add.98
  47.1 1.7 %collective-permute-start.1 = (f32[16,128]{1,0:T(8,128)S(1)}, f32[16,128]{1,0:T(8,128)S(1)}, u32[]{:S(2)}, u32[]{:S(2)}) collective-permute-start(f32[16,128]{1,0:T(8,128)S(1)} %add.98), channel_id=1, source_target_pairs={{0,2},{1,3},{2,0},{3,1},{4,6},{5,7},{6,4},{7,5},{8,10},{9,11},{10,... | collective-permute-start | bytes 24584 | tf_op jit(solution)/shard_map/ppermute | solution.py:68
  48.8 1.9 %collective-permute-done.1 = f32[16,128]{1,0:T(8,128)S(1)} collective-permute-done((f32[16,128]{1,0:T(8,128)S(1)}, f32[16,128]{1,0:T(8,128)S(1)}, u32[]{:S(2)}, u32[]{:S(2)}) %collective-permute-start.1) | collective-permute-done | bytes 8224 | tf_op jit(solution)/shard_map/ppermute | solution.py:68
  50.8 14.1 %all_gather.21 = f32[16,1024]{1,0:T(8,128)S(1)} all-gather(f32[16,128]{1,0:T(8,128)S(1)} %add.99), channel_id=1, replica_groups=mesh['wide'=8,'narrow'=4] {'wide'}, dimensions={1}, use_global_device_ids=true | all-gather | bytes 73728 | tf_op jit(solution)/shard_map/all_gather | solution.py:69
  64.9 0.9 fusion.13
  66.0 8.4 %all_gather.23 = f32[16,1024]{1,0:T(8,128)S(1)} all-gather(f32[16,256]{1,0:T(8,128)S(1)} %fusion.13), channel_id=1, replica_groups=mesh['wide'=8,'narrow'=4] {'narrow'}, dimensions={1}, use_global_device_ids=true | all-gather | bytes 81920 | tf_op jit(solution)/shard_map/all_gather | solution.py:58
  74.8 0.7 gather_fusion.2
  75.5 2.6 %collective-permute-done.2 = f32[16,128]{1,0:T(8,128)S(1)} collective-permute-done((f32[16,128]{1,0:T(8,128)S(1)}, f32[16,128]{1,0:T(8,128)S(1)}, u32[]{:S(2)}, u32[]{:S(2)}) %collective-permute-start.2) | collective-permute-done | bytes 8224 | tf_op jit(solution)/shard_map/ppermute | solution.py:68
  78.4 0.6 convolution_bitcast_fusion
  79.1 2.7 %collective-permute-done.3 = f32[16,128]{1,0:T(8,128)S(1)} collective-permute-done((f32[16,128]{1,0:T(8,128)S(1)}, f32[16,128]{1,0:T(8,128)S(1)}, u32[]{:S(2)}, u32[]{:S(2)}) %collective-permute-start.3) | collective-permute-done | bytes 8224 | tf_op jit(solution)/shard_map/ppermute | solution.py:68
  81.8 13.9 %all_gather.24 = f32[16,1024]{1,0:T(8,128)S(1)} all-gather(f32[16,128]{1,0:T(8,128)S(1)} %add.107), channel_id=1, replica_groups=mesh['wide'=8,'narrow'=4] {'wide'}, dimensions={1}, use_global_device_ids=true | all-gather | bytes 73728 | tf_op jit(solution)/shard_map/all_gather | solution.py:69
  95.7 1.5 %multiply_add_fusion = (f32[16,256]{1,0:T(8,128)}, f32[16,256]{1,0:T(8,128)}) fusion(f32[16,256]{1,0:T(8,128)S(1)} %fusion.13, f32[16,256]{1,0:T(8,128)S(1)} %copy-done.3, f32[256,1024]{1,0:T(8,128)S(1)} %fusion.2, f32[16,1024]{1,0:T(8,128)S(1)} %all_gather.24, pred[1024]{0:T(1024)(128)(4,1)S(1)} %fusion.20, f32[2,2,8,128]{3,2,1,0:T(8,128)S(1)} %convolution_bitcast_fusion), kind=kOutput, calls=%fused_computation.34 | convolution fusion | flops 50368512 | bytes 1197056 | tf_op jit(solution)/shard_map/while/body/eval_jaxpr/rs,ps->rp/dot_general | solution.py:29
  (39 shorter events, 3.4 us)
Async XLA Ops:
  0.6 0.9 copy-start
  0.6 5.4 %copy-start.1 = (f32[256,128]{1,0:T(8,128)S(1)}, f32[256,128]{1,0:T(8,128)}, u32[]{:S(2)}) copy-start(f32[256,128]{1,0:T(8,128)} %param.7) | copy-start | bytes 393220
  3.0 43.4 %collective-permute-start = (f32[16,128]{1,0:T(8,128)}, f32[16,128]{1,0:T(8,128)}, u32[]{:S(2)}, u32[]{:S(2)}) collective-permute-start(f32[16,128]{1,0:T(8,128)} %fusion.26), channel_id=1, source_target_pairs={{0,1},{1,0},{2,3},{3,2},{4,5},{5,4},{6,7},{7,6},{8,9},{9,8},{10,11... | collective-permute-start | bytes 24584 | tf_op jit(solution)/shard_map/ppermute | solution.py:68
  16.3 0.7 copy-start.2
  17.0 25.7 %copy-start.7 = (f32[256]{0:T(256)}, f32[256]{0:T(256)S(1)}, u32[]{:S(2)}) copy-start(f32[256]{0:T(256)S(1)} %multiply_reduce_fusion.2) | copy-start | bytes 3076
  17.0 7.2 %copy-start.10 = (s32[2,8]{1,0:T(2,128)S(1)}, s32[2,8]{1,0:T(2,128)}, u32[]{:S(2)}) copy-start(s32[2,8]{1,0:T(2,128)} %param.12) | copy-start | bytes 196
  24.3 2.2 %copy-start.6 = (s32[1024]{0:T(1024)}, s32[1024]{0:T(1024)S(1)}, u32[]{:S(2)}) copy-start(s32[1024]{0:T(1024)S(1)} %pad_clamp_fusion) | copy-start | bytes 12292
  24.9 1.0 copy-start.11
  26.5 0.8 copy-start.4
  42.7 1.2 %copy-start.5 = (f32[2,8,128]{2,1,0:T(8,128)S(1)}, f32[2,8,128]{2,1,0:T(8,128)}, u32[]{:S(2)}) copy-start(f32[2,8,128]{2,1,0:T(8,128)} %multiply_reduce_fusion) | copy-start | bytes 24580
  42.7 1.2 %copy-start.9 = (f32[2,8]{1,0:T(2,128)S(1)}, f32[2,8]{1,0:T(2,128)}, u32[]{:S(2)}) copy-start(f32[2,8]{1,0:T(2,128)} %compare_convert_fusion) | copy-start | bytes 196
  43.9 0.7 copy-start.8
  47.1 3.7 %collective-permute-start.1 = (f32[16,128]{1,0:T(8,128)S(1)}, f32[16,128]{1,0:T(8,128)S(1)}, u32[]{:S(2)}, u32[]{:S(2)}) collective-permute-start(f32[16,128]{1,0:T(8,128)S(1)} %add.98), channel_id=1, source_target_pairs={{0,2},{1,3},{2,0},{3,1},{4,6},{5,7},{6,4},{7,5},{8,10},{9,11},{10,... | collective-permute-start | bytes 24584 | tf_op jit(solution)/shard_map/ppermute | solution.py:68
  50.8 14.1 %copy-start.3 = (f32[16,256]{1,0:T(8,128)S(1)}, f32[16,256]{1,0:T(8,128)}, u32[]{:S(2)}) copy-start(f32[16,256]{1,0:T(8,128)} %param.8) | copy-start | bytes 49156
  74.4 3.7 %collective-permute-start.2 = (f32[16,128]{1,0:T(8,128)S(1)}, f32[16,128]{1,0:T(8,128)S(1)}, u32[]{:S(2)}, u32[]{:S(2)}) collective-permute-start(f32[16,128]{1,0:T(8,128)S(1)} %fusion.27), channel_id=1, source_target_pairs={{0,1},{1,0},{2,3},{3,2},{4,5},{5,4},{6,7},{7,6},{8,9},{9,8},{10,11... | collective-permute-start | bytes 24584 | tf_op jit(solution)/shard_map/ppermute | solution.py:68
  78.1 3.7 %collective-permute-start.3 = (f32[16,128]{1,0:T(8,128)S(1)}, f32[16,128]{1,0:T(8,128)S(1)}, u32[]{:S(2)}, u32[]{:S(2)}) collective-permute-start(f32[16,128]{1,0:T(8,128)S(1)} %add.106), channel_id=1, source_target_pairs={{0,2},{1,3},{2,0},{3,1},{4,6},{5,7},{6,4},{7,5},{8,10},{9,11},{10,... | collective-permute-start | bytes 24584 | tf_op jit(solution)/shard_map/ppermute | solution.py:68
